TPU v7x, 32 devices: a whole 2x2x4 slice. The times are simulated.
32 devices in a mesh: owner: 4 (over z), rows: 8 (over y, x, core).
Axes of the slice: x: 2, y: 2, z: 4, core: 2. Of those that a mesh axis runs over, the one named last changes fastest.
Arguments:
- w_gate: float32 [128, 2048, 768], P('owner', 'rows'), may hold values from -0.1875 to 0.1875
- w_up: float32 [128, 2048, 768], P('owner', 'rows'), may hold values from -0.1875 to 0.1875
- router_weight: float32 [2048, 128], P('rows', 'owner'), may hold values from -0.125 to 0.125
- router_gain: float32 [2048], P('rows'), may hold values from 0.25 to 1.75
Outputs:
- serve_gate: bfloat16 [128, 2048, 768], P('owner', None, 'rows')
- serve_up: bfloat16 [128, 2048, 768], P('owner', None, 'rows')
- scale_gate: float32 [128, 768], P('owner', 'rows')
- scale_up: float32 [128, 768], P('owner', 'rows')
- serve_router: bfloat16 [2048, 128], replicated
All inputs are finite; a program needn't handle non-finite values. Where the computation divides by a largest or mean magnitude, that divisor is 1e-20 or more.
Results may differ from a plain program's by a relative error of at most 0.001.
Values may be sent and summed in bfloat16 or wider, within the bound.
No kernel may reach another device: no remote copies, remote signals or barrier semaphores. Data moves between devices by JAX's collectives and lax.ppermute only.
A program may use at most 192 MiB of HBM per device.

v0:
```python
import jax
import jax.numpy as jnp
from jax import lax
from jax.sharding import PartitionSpec as P

D_MODEL = 2048


def on_device(w_gate, w_up, router_weight, router_gain):
    total_gate, total_up = lax.psum(
        (jnp.sum(jnp.abs(w_gate), axis=1), jnp.sum(jnp.abs(w_up), axis=1)), "rows"
    )
    scale_gate = total_gate / D_MODEL
    scale_up = total_up / D_MODEL
    narrow_gate, narrow_up = (
        (w_gate / jnp.expand_dims(scale_gate, 1)).astype(jnp.bfloat16),
        (w_up / jnp.expand_dims(scale_up, 1)).astype(jnp.bfloat16),
    )
    serve_gate, serve_up = (
        lax.all_to_all(narrow_gate, "rows", split_axis=2, concat_axis=1, tiled=True),
        lax.all_to_all(narrow_up, "rows", split_axis=2, concat_axis=1, tiled=True),
    )
    scale_gate = lax.dynamic_slice_in_dim(
        scale_gate, lax.axis_index("rows") * serve_gate.shape[2], serve_gate.shape[2], axis=1
    )
    scale_up = lax.dynamic_slice_in_dim(
        scale_up, lax.axis_index("rows") * serve_up.shape[2], serve_up.shape[2], axis=1
    )
    part_router = (router_weight * router_gain[:, None]).astype(jnp.bfloat16)
    row_router = lax.all_gather(part_router, "rows", axis=0, tiled=True)
    serve_router = lax.all_gather(row_router, "owner", axis=1, tiled=True)
    return (serve_gate, serve_up, scale_gate, scale_up, serve_router)


def solution(mesh):
    placed = (P("owner", "rows", None), P("owner", "rows", None), P("rows", "owner"), P("rows"))
    return jax.shard_map(
        on_device,
        mesh=mesh,
        in_specs=placed,
        out_specs=(
            P("owner", None, "rows"),
            P("owner", None, "rows"),
            P("owner", "rows"),
            P("owner", "rows"),
            P(),
        ),
        check_vma=False,
    )
```

profile of v0, /device:TPU:0, one launch (start us, length us, event | category | flops | bytes accessed | tf_op | source)
XLA Modules:
  0.0 481.1 jit_solution(11326135817132377053)
XLA Ops:
  7.2 0.0 all-reduce.3.cloned.1.call-start
  7.2 17.4 %abs_reduce_fusion = (f32[32,768]{1,0:T(8,128)}, f32[32,768]{1,0:T(8,128)}) fusion(f32[32,256,768]{2,1,0:T(8,128)} %param.5, f32[32,256,768]{2,1,0:T(8,128)} %param.4), kind=kLoop, calls=%fused_computation.1 | loop fusion | flops 25116672 | bytes 50528256 | tf_op jit(solution)/shard_map/reduce_sum | solution.py:11
  24.6 0.0 all-reduce.3.cloned.1.call-update
  24.7 25.1 %copy.25 = f32[32,256,768]{1,0,2:T(8,128)} copy(f32[32,256,768]{2,1,0:T(8,128)} %param.5) | data formatting | bytes 50331648 | tf_op args[1]
  49.8 31.5 %all-reduce.3.cloned.1.call-done = (f32[32,768]{1,0:T(8,128)}, f32[32,768]{1,0:T(8,128)}) async-done(((f32[32,768]{1,0:T(8,128)}, f32[32,768]{1,0:T(8,128)}), (f32[32,768]{1,0:T(8,128)}, f32[32,768]{1,0:T(8,128)})) %all-reduce.3.cloned.1.call-update) | async-done | bytes 196624 | tf_op jit(solution)/shard_map/psum | solution.py:10
  81.3 0.9 broadcast_multiply_fusion
  82.2 0.2 copy.24
  82.4 14.1 %divide_convert_fusion = bf16[32,256,768]{1,0,2:T(8,128)(2,1)} fusion(f32[32,256,768]{1,0,2:T(8,128)} %copy.25, f32[32,768]{0,1:T(8,128)S(1)} %copy.24), kind=kLoop, calls=%fused_computation | loop fusion | flops 12582912 | bytes 37847040 | tf_op jit(solution)/shard_map/convert_element_type | solution.py:17
  96.5 5.4 %all-to-all-start.1 = ((bf16[32,256,768]{1,0,2:T(8,128)(2,1)}), bf16[32,256,768]{1,0,2:T(8,128)(2,1)}, u32[]{:S(2)}, u32[]{:S(2)}) async-start(bf16[32,256,768]{1,0,2:T(8,128)(2,1)} %divide_convert_fusion), calls=%async_computation.1 | async-start | bytes 25165824 | tf_op jit(solution)/shard_map/all_to_all | solution.py:21
  101.9 0.0 copy-start
  101.9 25.1 %copy.21 = f32[32,256,768]{1,0,2:T(8,128)} copy(f32[32,256,768]{2,1,0:T(8,128)} %param.4) | data formatting | bytes 50331648 | tf_op args[0]
  127.1 0.0 copy-done
  127.1 0.2 copy.20
  127.2 0.0 copy-start.1
  127.3 0.0 copy-start.2
  127.3 14.1 %divide_convert_fusion.1 = bf16[32,256,768]{1,0,2:T(8,128)(2,1)} fusion(f32[32,256,768]{1,0,2:T(8,128)} %copy.21, f32[32,768]{0,1:T(8,128)S(1)} %copy.20), kind=kLoop, calls=%fused_computation.2 | loop fusion | flops 12582912 | bytes 37847040 | tf_op jit(solution)/shard_map/convert_element_type | solution.py:16
  141.4 99.5 %all-to-all-done.1 = bf16[32,256,768]{1,0,2:T(8,128)(2,1)} async-done(((bf16[32,256,768]{1,0,2:T(8,128)(2,1)}), bf16[32,256,768]{1,0,2:T(8,128)(2,1)}, u32[]{:S(2)}, u32[]{:S(2)}) %all-to-all-start.1) | async-done | bytes 12582944 | tf_op jit(solution)/shard_map/all_to_all | solution.py:21
  240.9 5.4 %all-to-all-start = ((bf16[32,256,768]{1,0,2:T(8,128)(2,1)}), bf16[32,256,768]{1,0,2:T(8,128)(2,1)}, u32[]{:S(2)}, u32[]{:S(2)}) async-start(bf16[32,256,768]{1,0,2:T(8,128)(2,1)} %divide_convert_fusion.1), calls=%async_computation | async-start | bytes 25165824 | tf_op jit(solution)/shard_map/all_to_all | solution.py:20
  246.3 0.0 copy-done.1
  246.3 0.0 copy-done.2
  246.3 142.4 %all_gather.6 = bf16[2048,32]{0,1:T(8,128)(2,1)S(1)} all-gather(bf16[256,32]{0,1:T(8,128)(2,1)S(1)} %multiply_convert_fusion), channel_id=1, replica_groups=mesh['owner'=4,'rows'=8] {'rows'}, dimensions={0}, use_global_device_ids=true | all-gather | bytes 147456 | tf_op jit(solution)/shard_map/all_gather | solution.py:30
  388.8 16.1 %all_gather.7 = bf16[2048,128]{0,1:T(8,128)(2,1)S(1)} all-gather(bf16[2048,32]{0,1:T(8,128)(2,1)S(1)} %all_gather.6), channel_id=1, replica_groups=mesh['owner'=4,'rows'=8] {'owner'}, dimensions={1}, use_global_device_ids=true | all-gather | bytes 655360 | tf_op jit(solution)/shard_map/all_gather | solution.py:31
  404.8 1.0 copy.28
  405.8 0.7 constant_dynamic-slice_fusion
  406.5 0.7 constant_dynamic-slice_fusion.1
  407.2 14.1 %copy.27 = bf16[32,8,256,96]{2,1,3,0:T(8,128)(2,1)} copy(bf16[32,8,256,96]{2,0,3,1:T(8,128)(2,1)} %bitcast.5) | data formatting | bytes 25165824 | tf_op jit(solution)/shard_map/all_to_all | solution.py:21
  421.2 19.5 %all_to_all.33 = bf16[32,2048,96]{1,2,0:T(8,128)(2,1)} reshape(bf16[32,8,256,96]{2,1,3,0:T(8,128)(2,1)} %copy.27) | data formatting | bytes 25165824 | tf_op jit(solution)/shard_map/all_to_all | solution.py:21
  440.7 0.0 all-to-all-done
  440.7 14.1 %copy.23 = bf16[32,8,256,96]{2,1,3,0:T(8,128)(2,1)} copy(bf16[32,8,256,96]{2,0,3,1:T(8,128)(2,1)} %bitcast.2) | data formatting | bytes 25165824 | tf_op jit(solution)/shard_map/all_to_all | solution.py:20
  454.8 19.5 %all_to_all.29 = bf16[32,2048,96]{1,2,0:T(8,128)(2,1)} reshape(bf16[32,8,256,96]{2,1,3,0:T(8,128)(2,1)} %copy.23) | data formatting | bytes 25165824 | tf_op jit(solution)/shard_map/all_to_all | solution.py:20
  (2 shorter events, 0.0 us)
Async XLA Ops:
  7.2 74.2 %all-reduce.3.cloned.1.call-start = ((), (), s32[]{:S(2)}) async-start(), calls=%async_computation.2 | async-start | bytes 393216 | tf_op jit(solution)/shard_map/psum | solution.py:10
  96.5 144.4 %all-to-all-start.1 = ((bf16[32,256,768]{1,0,2:T(8,128)(2,1)}), bf16[32,256,768]{1,0,2:T(8,128)(2,1)}, u32[]{:S(2)}, u32[]{:S(2)}) async-start(bf16[32,256,768]{1,0,2:T(8,128)(2,1)} %divide_convert_fusion), calls=%async_computation.1 | async-start | bytes 25165824 | tf_op jit(solution)/shard_map/all_to_all | solution.py:21
  101.9 25.1 %copy-start = (f32[32,768]{1,0:T(8,128)S(1)}, f32[32,768]{1,0:T(8,128)}, u32[]{:S(2)}) copy-start(f32[32,768]{1,0:T(8,128)} %get-tuple-element.10) | copy-start | bytes 294916
  127.2 119.0 %copy-start.1 = (f32[256,32]{0,1:T(8,128)S(1)}, f32[256,32]{0,1:T(8,128)}, u32[]{:S(2)}) copy-start(f32[256,32]{0,1:T(8,128)} %param.6) | copy-start | bytes 98308
  127.3 119.0 %copy-start.2 = (f32[256]{0:T(256)S(1)}, f32[256]{0:T(256)}, u32[]{:S(2)}) copy-start(f32[256]{0:T(256)} %param.7) | copy-start | bytes 3076
  240.9 199.8 %all-to-all-start = ((bf16[32,256,768]{1,0,2:T(8,128)(2,1)}), bf16[32,256,768]{1,0,2:T(8,128)(2,1)}, u32[]{:S(2)}, u32[]{:S(2)}) async-start(bf16[32,256,768]{1,0,2:T(8,128)(2,1)} %divide_convert_fusion.1), calls=%async_computation | async-start | bytes 25165824 | tf_op jit(solution)/shard_map/all_to_all | solution.py:20
Sparse Core Ops, SparseCore 0:
  24.8 56.4 all-reduce.2
where the time goes:
time: 483 us; the launch traced here: 481 us
  blocking collectives  158 us (33%)
  waiting for transfers between devices  131 us (27%)
  local copies, waits for them, and re-layouts  120 us (25%)
  other arithmetic  46.6 us (10%)
  between operations  14.1 us (3%)
  starting transfers between devices  10.8 us (2%)
    all_gather x1, blocking collectives, on_device(): row_router = lax.all_gather(part_router, 'rows', axis=0, tiled=True)  142 us
    all_to_all x1, waiting for transfers between devices, on_device(): lax.all_to_all(narrow_up, 'rows', split_axis=2, concat_axis=1, tiled=True)  99.5 us
    unnamed x9, local copies, waits for them, and re-layouts  51.3 us
    all_to_all x2, local copies, waits for them, and re-layouts, on_device(): lax.all_to_all(narrow_gate, 'rows', split_axis=2, concat_axis=1, tiled=True)  33.6 us
    all_to_all x2, local copies, waits for them, and re-layouts, on_device(): lax.all_to_all(narrow_up, 'rows', split_axis=2, concat_axis=1, tiled=True)  33.6 us
    psum x1, waiting for transfers between devices, on_device(): lax.psum((jnp.sum(jnp.abs(w_gate), axis=1), jnp.sum(jnp.abs(w_up), axis=1...  31.5 us
    reduce_sum x1, other arithmetic, on_device(): jnp.sum(jnp.abs(w_up), axis=1)  17.4 us
    all_gather x1, blocking collectives, on_device(): serve_router = lax.all_gather(row_router, 'owner', axis=1, tiled=True)  16.1 us
  transfers between devices with their start and end apart: 3, of which 2 were waited for; matrix products, arithmetic and copies ran while one was open for 17% of the time, Pallas kernels for 0%

commit v1 on v0

--- a/solution.py
+++ b/solution.py
@@ -4,6 +4,22 @@
 from jax.sharding import PartitionSpec as P
 
 D_MODEL = 2048
+
+
+def members_all_group(xs, axis_tag, join_dim):
+    q_n = jax.lax.psum(1, axis_tag)
+    passed = xs
+    all_rows = list(map(lambda rr: (rr - 1, rr), range(1, q_n))) + [(q_n - 1, 0)]
+    b = 0
+    row_list = [passed]
+    while b < q_n - 1:
+        passed = jax.lax.ppermute(passed, axis_tag, all_rows)
+        row_list += [passed]
+        b += 1
+    after = jnp.concatenate([*reversed(row_list)], join_dim)
+    return jnp.roll(
+        after, shift=(jax.lax.axis_index(axis_tag) + 1) * passed.shape[join_dim], axis=join_dim
+    )
 
 
 def on_device(w_gate, w_up, router_weight, router_gain):
@@ -27,7 +43,7 @@
         scale_up, lax.axis_index("rows") * serve_up.shape[2], serve_up.shape[2], axis=1
     )
     part_router = (router_weight * router_gain[:, None]).astype(jnp.bfloat16)
-    row_router = lax.all_gather(part_router, "rows", axis=0, tiled=True)
+    row_router = members_all_group(part_router, "rows", join_dim=0)
     serve_router = lax.all_gather(row_router, "owner", axis=1, tiled=True)
     return (serve_gate, serve_up, scale_gate, scale_up, serve_router)
 

time: 483 us -> 503 us (1.041)
  waiting for transfers between devices: 131 us -> 292 us
  blocking collectives: 158 us -> 16.2 us
    ppermute x0 -> x7, waiting for transfers between devices: none -> 161 us  [members_all_group(): passed = jax.lax.ppermute(passed, axis_tag, all_rows)]
    all_gather x1 -> x0, blocking collectives: 142 us -> none  [on_device(): row_router = lax.all_gather(part_router, 'rows', axis=0, tiled=True)]
    all_to_all x1, waiting for transfers between devices: 0.01 us -> 99.6 us  [on_device(): lax.all_to_all(narrow_gate, 'rows', split_axis=2, concat_axis=1, tiled=True)]
    all_to_all x1, waiting for transfers between devices: 99.5 us -> 0.01 us  [on_device(): lax.all_to_all(narrow_up, 'rows', split_axis=2, concat_axis=1, tiled=True)]
    unnamed x9 -> x23, local copies, waits for them, and re-layouts: 51.3 us -> 51.2 us
  transfers between devices with their start and end apart: 3 -> 10, of which waited for: 2 -> 9; matrix products, arithmetic and copies ran while one was open for 17% -> 16% of each run, Pallas kernels for 0% -> 0%
where the time goes in v1:
time: 503 us; the launch traced here: 501 us
  waiting for transfers between devices  292 us (58%)
  local copies, waits for them, and re-layouts  120 us (24%)
  other arithmetic  46.6 us (9%)
  blocking collectives  16.2 us (3%)
  between operations  14.2 us (3%)
  starting transfers between devices  11.2 us (2%)
    ppermute x7, waiting for transfers between devices, members_all_group(): passed = jax.lax.ppermute(passed, axis_tag, all_rows)  161 us
    all_to_all x1, waiting for transfers between devices, on_device(): lax.all_to_all(narrow_gate, 'rows', split_axis=2, concat_axis=1, tiled=True)  99.6 us
    unnamed x23, local copies, waits for them, and re-layouts  51.2 us
    all_to_all x2, local copies, waits for them, and re-layouts, on_device(): lax.all_to_all(narrow_gate, 'rows', split_axis=2, concat_axis=1, tiled=True)  33.5 us
    all_to_all x2, local copies, waits for them, and re-layouts, on_device(): lax.all_to_all(narrow_up, 'rows', split_axis=2, concat_axis=1, tiled=True)  33.5 us
    psum x1, waiting for transfers between devices, on_device(): lax.psum((jnp.sum(jnp.abs(w_gate), axis=1), jnp.sum(jnp.abs(w_up), axis=1...  31.6 us
    reduce_sum x1, other arithmetic, on_device(): jnp.sum(jnp.abs(w_up), axis=1)  17.4 us
    all_gather x1, blocking collectives, on_device(): serve_router = lax.all_gather(row_router, 'owner', axis=1, tiled=True)  16.2 us
  transfers between devices with their start and end apart: 10, of which 9 were waited for; matrix products, arithmetic and copies ran while one was open for 16% of the time, Pallas kernels for 0%

profile of v1, /device:TPU:0, one launch (start us, length us, event | category | flops | bytes accessed | tf_op | source)
XLA Modules:
  0.0 500.6 jit_solution(17368511541042503295)
XLA Ops:
  7.2 0.0 all-reduce.3.cloned.1.call-start
  7.2 17.4 %abs_reduce_fusion = (f32[32,768]{1,0:T(8,128)}, f32[32,768]{1,0:T(8,128)}) fusion(f32[32,256,768]{2,1,0:T(8,128)} %param.5, f32[32,256,768]{2,1,0:T(8,128)} %param.4), kind=kLoop, calls=%fused_computation.1 | loop fusion | flops 25116672 | bytes 50528256 | tf_op jit(solution)/shard_map/reduce_sum | solution.py:27
  24.6 0.0 all-reduce.3.cloned.1.call-update
  24.7 25.0 %copy.21 = f32[32,256,768]{1,0,2:T(8,128)} copy(f32[32,256,768]{2,1,0:T(8,128)} %param.4) | data formatting | bytes 50331648 | tf_op args[0]
  49.7 31.6 %all-reduce.3.cloned.1.call-done = (f32[32,768]{1,0:T(8,128)}, f32[32,768]{1,0:T(8,128)}) async-done(((f32[32,768]{1,0:T(8,128)}, f32[32,768]{1,0:T(8,128)}), (f32[32,768]{1,0:T(8,128)}, f32[32,768]{1,0:T(8,128)})) %all-reduce.3.cloned.1.call-update) | async-done | bytes 196624 | tf_op jit(solution)/shard_map/psum | solution.py:26
  81.3 0.9 broadcast_multiply_fusion.1
  82.2 0.2 copy.20
  82.4 14.1 %divide_convert_fusion.1 = bf16[32,256,768]{1,0,2:T(8,128)(2,1)} fusion(f32[32,256,768]{1,0,2:T(8,128)} %copy.21, f32[32,768]{0,1:T(8,128)S(1)} %copy.20), kind=kLoop, calls=%fused_computation.2 | loop fusion | flops 12582912 | bytes 37847040 | tf_op jit(solution)/shard_map/convert_element_type | solution.py:32
  96.5 5.4 %all-to-all-start = ((bf16[32,256,768]{1,0,2:T(8,128)(2,1)}), bf16[32,256,768]{1,0,2:T(8,128)(2,1)}, u32[]{:S(2)}, u32[]{:S(2)}) async-start(bf16[32,256,768]{1,0,2:T(8,128)(2,1)} %divide_convert_fusion.1), calls=%async_computation | async-start | bytes 25165824 | tf_op jit(solution)/shard_map/all_to_all | solution.py:36
  101.9 0.0 copy-start.1
  101.9 25.1 %copy.25 = f32[32,256,768]{1,0,2:T(8,128)} copy(f32[32,256,768]{2,1,0:T(8,128)} %param.5) | data formatting | bytes 50331648 | tf_op args[1]
  127.0 0.0 copy-done.1
  127.0 0.2 copy.24
  127.2 0.0 copy-start
  127.2 0.0 copy-start.2
  127.2 14.1 %divide_convert_fusion = bf16[32,256,768]{1,0,2:T(8,128)(2,1)} fusion(f32[32,256,768]{1,0,2:T(8,128)} %copy.25, f32[32,768]{0,1:T(8,128)S(1)} %copy.24), kind=kLoop, calls=%fused_computation | loop fusion | flops 12582912 | bytes 37847040 | tf_op jit(solution)/shard_map/convert_element_type | solution.py:33
  141.3 99.6 %all-to-all-done = bf16[32,256,768]{1,0,2:T(8,128)(2,1)} async-done(((bf16[32,256,768]{1,0,2:T(8,128)(2,1)}), bf16[32,256,768]{1,0,2:T(8,128)(2,1)}, u32[]{:S(2)}, u32[]{:S(2)}) %all-to-all-start) | async-done | bytes 12582944 | tf_op jit(solution)/shard_map/all_to_all | solution.py:36
  240.9 5.3 %all-to-all-start.1 = ((bf16[32,256,768]{1,0,2:T(8,128)(2,1)}), bf16[32,256,768]{1,0,2:T(8,128)(2,1)}, u32[]{:S(2)}, u32[]{:S(2)}) async-start(bf16[32,256,768]{1,0,2:T(8,128)(2,1)} %divide_convert_fusion), calls=%async_computation.1 | async-start | bytes 25165824 | tf_op jit(solution)/shard_map/all_to_all | solution.py:37
  246.2 0.0 copy-done
  246.2 0.0 copy-done.2
  246.3 0.4 collective-permute-start
  246.7 138.2 %collective-permute-done = bf16[256,32]{0,1:T(8,128)(2,1)S(1)} collective-permute-done((bf16[256,32]{0,1:T(8,128)(2,1)S(1)}, bf16[256,32]{0,1:T(8,128)(2,1)S(1)}, u32[]{:S(2)}, u32[]{:S(2)}) %collective-permute-start) | collective-permute-done | bytes 16416 | tf_op jit(solution)/shard_map/ppermute | solution.py:16
  384.9 0.0 collective-permute-start.1
  384.9 4.1 collective-permute-done.1
  388.9 0.0 collective-permute-start.2
  389.0 4.1 collective-permute-done.2
  393.0 0.0 collective-permute-start.3
  393.0 4.1 collective-permute-done.3
  397.1 0.0 collective-permute-start.4
  397.1 4.1 collective-permute-done.4
  401.1 0.0 collective-permute-start.5
  401.1 4.1 collective-permute-done.5
  405.2 0.0 collective-permute-start.6
  405.2 0.7 constant_dynamic-slice_fusion.2
  405.9 0.7 constant_dynamic-slice_fusion.1
  406.6 2.7 collective-permute-done.6
  409.5 16.2 %all_gather.3 = bf16[2048,128]{0,1:T(8,128)(2,1)S(1)} all-gather(bf16[2048,32]{0,1:T(8,128)(2,1)S(1)} %constant_dynamic-slice_fusion), channel_id=1, replica_groups=mesh['owner'=4,'rows'=8] {'owner'}, dimensions={1}, use_global_device_ids=true | all-gather | bytes 655360 | tf_op jit(solution)/shard_map/all_gather | solution.py:47
  425.6 1.0 copy.28
  426.6 14.1 %copy.23 = bf16[32,8,256,96]{2,1,3,0:T(8,128)(2,1)} copy(bf16[32,8,256,96]{2,0,3,1:T(8,128)(2,1)} %bitcast.2) | data formatting | bytes 25165824 | tf_op jit(solution)/shard_map/all_to_all | solution.py:36
  440.7 19.5 %all_to_all.29 = bf16[32,2048,96]{1,2,0:T(8,128)(2,1)} reshape(bf16[32,8,256,96]{2,1,3,0:T(8,128)(2,1)} %copy.23) | data formatting | bytes 25165824 | tf_op jit(solution)/shard_map/all_to_all | solution.py:36
  460.2 0.0 all-to-all-done.1
  460.2 14.1 %copy.27 = bf16[32,8,256,96]{2,1,3,0:T(8,128)(2,1)} copy(bf16[32,8,256,96]{2,0,3,1:T(8,128)(2,1)} %bitcast.5) | data formatting | bytes 25165824 | tf_op jit(solution)/shard_map/all_to_all | solution.py:37
  474.2 19.5 %all_to_all.33 = bf16[32,2048,96]{1,2,0:T(8,128)(2,1)} reshape(bf16[32,8,256,96]{2,1,3,0:T(8,128)(2,1)} %copy.27) | data formatting | bytes 25165824 | tf_op jit(solution)/shard_map/all_to_all | solution.py:37
  (19 shorter events, 0.1 us)
Async XLA Ops:
  7.2 74.2 %all-reduce.3.cloned.1.call-start = ((), (), s32[]{:S(2)}) async-start(), calls=%async_computation.2 | async-start | bytes 393216 | tf_op jit(solution)/shard_map/psum | solution.py:26
  96.5 144.4 %all-to-all-start = ((bf16[32,256,768]{1,0,2:T(8,128)(2,1)}), bf16[32,256,768]{1,0,2:T(8,128)(2,1)}, u32[]{:S(2)}, u32[]{:S(2)}) async-start(bf16[32,256,768]{1,0,2:T(8,128)(2,1)} %divide_convert_fusion.1), calls=%async_computation | async-start | bytes 25165824 | tf_op jit(solution)/shard_map/all_to_all | solution.py:36
  101.9 25.1 %copy-start.1 = (f32[32,768]{1,0:T(8,128)S(1)}, f32[32,768]{1,0:T(8,128)}, u32[]{:S(2)}) copy-start(f32[32,768]{1,0:T(8,128)} %get-tuple-element.11) | copy-start | bytes 294916
  127.2 119.1 %copy-start = (f32[256,32]{0,1:T(8,128)S(1)}, f32[256,32]{0,1:T(8,128)}, u32[]{:S(2)}) copy-start(f32[256,32]{0,1:T(8,128)} %param.6) | copy-start | bytes 98308
  127.2 119.1 %copy-start.2 = (f32[256]{0:T(256)S(1)}, f32[256]{0:T(256)}, u32[]{:S(2)}) copy-start(f32[256]{0:T(256)} %param.7) | copy-start | bytes 3076
  240.9 219.3 %all-to-all-start.1 = ((bf16[32,256,768]{1,0,2:T(8,128)(2,1)}), bf16[32,256,768]{1,0,2:T(8,128)(2,1)}, u32[]{:S(2)}, u32[]{:S(2)}) async-start(bf16[32,256,768]{1,0,2:T(8,128)(2,1)} %divide_convert_fusion), calls=%async_computation.1 | async-start | bytes 25165824 | tf_op jit(solution)/shard_map/all_to_all | solution.py:37
  246.3 138.6 %collective-permute-start = (bf16[256,32]{0,1:T(8,128)(2,1)S(1)}, bf16[256,32]{0,1:T(8,128)(2,1)S(1)}, u32[]{:S(2)}, u32[]{:S(2)}) collective-permute-start(bf16[256,32]{0,1:T(8,128)(2,1)S(1)} %multiply_convert_fusion), channel_id=1, source_target_pairs={{0,1},{1,2},{2,3},{3,4},{4,5},{5,6},{6,7},{7,0},{8,9},{9,10},{10,1... | collective-permute-start | bytes 49160 | tf_op jit(solution)/shard_map/ppermute | solution.py:16
  384.9 4.1 collective-permute-start.1
  388.9 4.1 collective-permute-start.2
  393.0 4.1 collective-permute-start.3
  397.1 4.1 collective-permute-start.4
  401.1 4.1 collective-permute-start.5
  405.2 4.1 collective-permute-start.6
Sparse Core Ops, SparseCore 0:
  24.8 56.4 all-reduce.2
